TPU v7x, 32 devices: a whole 2x2x4 slice. The times are simulated.
32 devices in a mesh: row: 16 (over z, y, x), col: 2 (over core).
Axes of the slice: x: 2, y: 2, z: 4, core: 2. Of those that a mesh axis runs over, the one named last changes fastest.
Arguments:
- centroids: float32 [3, 14336], P(None, ('row', 'col')), may hold values from -6 to 6
- normals: float32 [3, 14336], P(None, ('col', 'row')), may hold values from -6 to 6
- nodes: float32 [18, 14336], P(None, ('col', 'row')), may hold values from -6 to 6
- weights: float32 [6, 14336], P(None, ('col', 'row')), may hold values from 0.25 to 1
- row_scale: float32 [14336], P('row'), may hold values from 0.5 to 2
- col_scale: float32 [14336], P('col'), may hold values from 0.5 to 2
Outputs:
- transformed: float32 [14336, 14336], P('row', 'col')
All inputs are finite; a program needn't handle non-finite values.
Results may differ from a plain program's by a relative error of at most 0.0003.
Values sent between devices are 32-bit elements; how exact they have to be, the bound alone decides.
A program may use at most 128 MiB of HBM per device.

v0:
```python
import math

import jax
import jax.numpy as jnp
from jax import lax
from jax.sharding import PartitionSpec as P

core_square = 0.0625
kernel_scale = 1.0 / (4.0 * math.pi)
butterfly_scale = 1.0 / math.sqrt(2.0)


def from_partner(value, axis, distance):
    mask = 2**distance
    pairs = [(source, source ^ mask) for source in range(lax.axis_size(axis))]
    return lax.ppermute(value, axis, pairs)


def assemble(targets, panel_table, row_start, col_start):
    count = (panel_table.shape[0] - 3) // 4
    height = targets.shape[1]
    breadth = panel_table.shape[1]
    total = jnp.zeros((height, breadth), jnp.float32)
    for which in range(count):
        along_x = targets[0][:, None] - panel_table[3 + 3 * which][None, :]
        along_y = targets[1][:, None] - panel_table[4 + 3 * which][None, :]
        along_z = targets[2][:, None] - panel_table[5 + 3 * which][None, :]
        distance = along_x * along_x + along_y * along_y + along_z * along_z + core_square
        normal_dot = (
            panel_table[0][None, :] * along_x
            + panel_table[1][None, :] * along_y
            + panel_table[2][None, :] * along_z
        )
        total = (
            total
            + panel_table[3 + 3 * count + which][None, :]
            * normal_dot
            * lax.rsqrt(distance)
            / distance
        )
    row_ids = row_start + jnp.arange(height, dtype=jnp.int32)
    col_ids = col_start + jnp.arange(breadth, dtype=jnp.int32)
    return total * kernel_scale + jnp.where(row_ids[:, None] == col_ids[None, :], 0.5, 0.0)


def blend(partner, own, gain, sign):
    return gain * (partner + sign * own) * butterfly_scale


def per_device(centroids, normals, nodes, weights, row_scale, col_scale):
    targets = lax.all_gather(centroids, "col", axis=1, tiled=True)
    gathered = (
        lax.all_gather(normals, "row", axis=1, tiled=True),
        lax.all_gather(nodes, "row", axis=1, tiled=True),
        lax.all_gather(weights, "row", axis=1, tiled=True),
    )
    panel_table = jnp.concatenate(gathered, 0)
    height = targets.shape[1]
    breadth = panel_table.shape[1]
    row_pos = lax.axis_index("row")
    col_pos = lax.axis_index("col")
    half_row = lax.axis_size("row") // 2
    half_col = lax.axis_size("col") // 2
    row_bit = half_row.bit_length() - 1
    col_bit = half_col.bit_length() - 1
    row_start = row_pos * height
    col_start = col_pos * breadth
    far_row = jnp.bitwise_xor(row_pos, half_row) * height
    row_sign = jnp.where(row_pos < half_row, 1.0, -1.0).astype(jnp.float32)
    col_sign = jnp.where(col_pos < half_col, 1.0, -1.0).astype(jnp.float32)
    row_gain = row_scale[:, None]
    col_gain = col_scale[None, :]
    own = assemble(targets, panel_table, row_start, col_start)
    partner_targets = from_partner(targets, "row", row_bit)
    above = assemble(partner_targets, panel_table, far_row, col_start)
    mixed = blend(above, own, row_gain, row_sign)
    across = from_partner(mixed, "col", col_bit)
    return blend(across, mixed, col_gain, col_sign)


def solution(mesh):
    placed = (
        P(None, ("row", "col")),
        P(None, ("col", "row")),
        P(None, ("col", "row")),
        P(None, ("col", "row")),
        P("row"),
        P("col"),
    )
    return jax.shard_map(
        per_device, mesh=mesh, in_specs=placed, out_specs=P("row", "col"), check_vma=False
    )
```

profile of v0, /device:TPU:0, one launch (start us, length us, event | category | flops | bytes accessed | tf_op | source)
XLA Modules:
  0.0 412.7 jit_solution(16380364806824547754)
XLA Ops:
  0.0 2.2 all-gather.2
  2.2 0.1 reshape.25
  2.3 3.9 collective-permute-start
  6.3 39.7 %all-gather.1 = f32[16,448,3]{1,2,0:T(4,128)S(1)} all-gather(f32[1,448,3]{1,2,0:T(4,128)} %bitcast.86), channel_id=1, replica_groups=mesh['row'=16,'col'=2] {'row'}, dimensions={0}, use_global_device_ids=true | all-gather | bytes 91392 | tf_op jit(solution)/shard_map/all_gather | solution.py:53
  46.0 0.1 reshape.23
  46.1 0.1 fusion.108
  46.2 37.2 %all-gather = f32[16,448,6]{1,2,0:T(8,128)S(1)} all-gather(f32[1,448,6]{1,2,0:T(8,128)} %bitcast.84), channel_id=1, replica_groups=mesh['row'=16,'col'=2] {'row'}, dimensions={0}, use_global_device_ids=true | all-gather | bytes 182784 | tf_op jit(solution)/shard_map/all_gather | solution.py:55
  83.4 0.1 copy.11
  83.5 0.1 reshape.21
  83.6 0.1 fusion.107
  83.7 42.8 %all-gather.3 = f32[16,448,18]{1,2,0:T(8,128)S(1)} all-gather(f32[1,448,18]{1,2,0:T(8,128)} %bitcast.54), channel_id=1, replica_groups=mesh['row'=16,'col'=2] {'row'}, dimensions={0}, use_global_device_ids=true | all-gather | bytes 548352 | tf_op jit(solution)/shard_map/all_gather | solution.py:54
  126.5 0.3 copy.14
  126.9 0.3 reshape.27
  127.1 0.3 fusion.106
  127.5 0.0 collective-permute-done
  127.5 0.0 copy-start
  127.6 218.8 %broadcast_multiply_fusion = (f32[896,7168]{1,0:T(8,128)}, f32[896,7168]{1,0:T(8,128)}) fusion(s32[896]{0:T(1024)S(1)} %get-tuple-element.40, f32[896]{0:T(1024)S(1)} %get-tuple-element.9, f32[896]{0:T(1024)S(1)} %get-tuple-element.10, f32[896]{0:T(1024)S(1)} %get-tuple-element.8, f32[]{:T(128)S(6)} %select_n.15, s32[7168]{0:T(1024)S(1)} %iota_add_fusion, ...), kind=kLoop, calls=%fused_computation.180 | loop fusion | flops 1451491328 | bytes 52215300 | tf_op jit(solution)/shard_map/mul | solution.py:47
  346.4 0.1 collective-permute-start.1
  346.5 38.2 %collective-permute-done.1 = f32[896,7168]{1,0:T(8,128)} collective-permute-done((f32[896,7168]{1,0:T(8,128)}, f32[896,7168]{1,0:T(8,128)}, u32[]{:S(2)}, u32[]{:S(2)}) %collective-permute-start.1) | collective-permute-done | bytes 25690144 | tf_op jit(solution)/shard_map/ppermute | solution.py:16
  384.7 0.0 copy-done
  384.7 28.0 %multiply_multiply_fusion = f32[896,7168]{1,0:T(8,128)} fusion(f32[896,7168]{1,0:T(8,128)} %collective-permute-done.1, f32[896,7168]{1,0:T(8,128)} %get-tuple-element.12, f32[]{:T(128)S(6)} %mul.644, f32[7168]{0:T(1024)S(1)} %copy-done), kind=kLoop, calls=%fused_computation.178 | loop fusion | flops 25690112 | bytes 77099008 | tf_op jit(solution)/shard_map/mul | solution.py:47
  (6 shorter events, 0.1 us)
Async XLA Ops:
  2.3 125.2 %collective-permute-start = (f32[3,896]{1,0:T(4,128)S(1)}, f32[3,896]{1,0:T(4,128)S(1)}, u32[]{:S(2)}, u32[]{:S(2)}) collective-permute-start(f32[3,896]{1,0:T(4,128)S(1)} %bitcast.55), channel_id=1, source_target_pairs={{0,16},{2,18},{4,20},{6,22},{8,24},{10,26},{12,28},{14,30},{16,0},... | collective-permute-start | bytes 32264 | tf_op jit(solution)/shard_map/ppermute | solution.py:16
  127.5 257.2 %copy-start = (f32[7168]{0:T(1024)S(1)}, f32[7168]{0:T(1024)}, u32[]{:S(2)}) copy-start(f32[7168]{0:T(1024)} %param.11) | copy-start | bytes 86020
  346.4 38.3 %collective-permute-start.1 = (f32[896,7168]{1,0:T(8,128)}, f32[896,7168]{1,0:T(8,128)}, u32[]{:S(2)}, u32[]{:S(2)}) collective-permute-start(f32[896,7168]{1,0:T(8,128)} %get-tuple-element.11), channel_id=1, source_target_pairs={{0,1},{1,0},{2,3},{3,2},{4,5},{5,4},{6,7},{7,6},{8,9},{9,8},{10,11... | collective-permute-start | bytes 77070344 | tf_op jit(solution)/shard_map/ppermute | solution.py:16
where the time goes:
time: 413 us
  other arithmetic  247 us (60%)
  blocking collectives  122 us (30%)
  waiting for transfers between devices  38.2 us (9%)
    mul x2, other arithmetic, blend(): return gain * (partner + sign * own) * butterfly_scale  247 us
    all_gather x1, blocking collectives, per_device(): lax.all_gather(nodes, 'row', axis=1, tiled=True)  42.8 us
    all_gather x1, blocking collectives, per_device(): lax.all_gather(normals, 'row', axis=1, tiled=True)  39.7 us
    ppermute x2, waiting for transfers between devices, from_partner(): return lax.ppermute(value, axis, pairs)  38.2 us
    all_gather x1, blocking collectives, per_device(): lax.all_gather(weights, 'row', axis=1, tiled=True)  37.2 us
  transfers between devices with their start and end apart: 2, of which 1 were waited for; matrix products, arithmetic and copies ran while one was open for 0% of the time, Pallas kernels for 0%

commit v1 on v0

v1 whole, which is shorter than its diff:
```python
import functools
import math

import jax
import jax.numpy as jnp
from jax import lax
from jax.experimental import pallas as pl
from jax.experimental.pallas import tpu as pltpu
from jax.sharding import PartitionSpec as P

core_square = 0.0625
kernel_scale = 1.0 / (4.0 * math.pi)
MESH = pl.DeviceIdType.MESH
SUB = 32
LIMIT = 60 * 1024 * 1024
SPLITS = (0, 0, 0, 1, 1, 2)
SLOTS = [(piece, axis) for axis in range(4) for piece in SPLITS] + [(0, 4)] * 3


def gather_body(
    rows, cores, normals, nodes, weights, centroids, table, near,
    x_ref, g_ref, send_sem, recv_sem, pass_sem, take_sem,
):
    me = lax.axis_index("row")
    core = lax.axis_index("col")
    side = core // (cores // 2)
    other = lax.rem(core + cores // 2, cores)
    count = weights.shape[0]
    x_ref[...] = jnp.ones_like(x_ref)
    for axis in range(3):
        for which in range(count):
            row = 3 * which + axis
            x_ref[8 * axis + which : 8 * axis + which + 1, :] = nodes[row : row + 1, :]
        x_ref[8 * axis + 6 : 8 * axis + 7, :] = normals[axis : axis + 1, :]
        x_ref[8 * axis + 7 : 8 * axis + 8, :] = centroids[axis : axis + 1, :]
    x_ref[24 : 24 + count, :] = weights[...]

    barrier = pltpu.get_barrier_semaphore()
    for step in range(1, rows):
        pl.semaphore_signal(
            barrier, inc=1, device_id=(lax.rem(me + step, rows), core), device_id_type=MESH
        )
    pl.semaphore_signal(barrier, inc=1, device_id=(me, other), device_id_type=MESH)
    pl.semaphore_wait(barrier, rows)

    sends = []
    for step in range(1, rows):
        copy = pltpu.make_async_remote_copy(
            src_ref=x_ref,
            dst_ref=g_ref.at[me, side],
            send_sem=send_sem.at[step],
            recv_sem=recv_sem.at[step],
            device_id=(lax.rem(me + step, rows), core),
            device_id_type=MESH,
        )
        copy.start()
        sends.append(copy)
    passes = []
    first = pltpu.make_async_remote_copy(
        src_ref=x_ref,
        dst_ref=g_ref.at[me, side],
        send_sem=pass_sem.at[0],
        recv_sem=take_sem.at[0],
        device_id=(me, other),
        device_id_type=MESH,
    )
    first.start()
    passes.append(first)
    g_ref[me, side] = x_ref[...]
    for step in range(1, rows):
        sends[step - 1].wait_recv()
        source = lax.rem(me + rows - step, rows)
        copy = pltpu.make_async_remote_copy(
            src_ref=g_ref.at[source, side],
            dst_ref=g_ref.at[source, side],
            send_sem=pass_sem.at[step],
            recv_sem=take_sem.at[step],
            device_id=(me, other),
            device_id_type=MESH,
        )
        copy.start()
        passes.append(copy)
    for copy in sends:
        copy.wait_send()
    for copy in passes:
        copy.wait()
    width = x_ref.shape[1]
    for part in range(2):
        for source in range(rows):
            start = (part * rows + source) * width
            table[:, start : start + width] = g_ref[source, part]
    low = lax.rem(me, rows // 2)
    for part in range(2):
        for axis in range(3):
            near[part, axis : axis + 1, :] = g_ref[
                low + part * (rows // 2), side, 8 * axis + 7 : 8 * axis + 8, :
            ]


def gather(normals, nodes, weights, centroids):
    rows = lax.axis_size("row")
    cores = lax.axis_size("col")
    width = normals.shape[1]
    return pl.pallas_call(
        functools.partial(gather_body, rows, cores),
        out_shape=[
            jax.ShapeDtypeStruct((32, 2 * rows * width), jnp.float32),
            jax.ShapeDtypeStruct((2, 3, width), jnp.float32),
        ],
        in_specs=[pl.BlockSpec(memory_space=pltpu.VMEM)] * 4,
        out_specs=[pl.BlockSpec(memory_space=pltpu.VMEM)] * 2,
        scratch_shapes=[
            pltpu.VMEM((32, width), jnp.float32),
            pltpu.VMEM((rows, 2, 32, width), jnp.float32),
            pltpu.SemaphoreType.DMA((rows,)),
            pltpu.SemaphoreType.DMA((rows,)),
            pltpu.SemaphoreType.DMA((rows,)),
            pltpu.SemaphoreType.DMA((rows,)),
        ],
        compiler_params=pltpu.CompilerParams(
            collective_id=0, has_side_effects=True, vmem_limit_bytes=LIMIT
        ),
        name="gather",
    )(normals, nodes, weights, centroids)


def pieces(value):
    one = value.astype(jnp.bfloat16).astype(jnp.float32)
    rest = value - one
    two = rest.astype(jnp.bfloat16).astype(jnp.float32)
    return one, two, rest - two


def panel_rows(count, table):
    x, y, z, weight = table[0:8, :], table[8:16, :], table[16:24, :], table[24:32, :]
    row = lax.broadcasted_iota(jnp.int32, x.shape, 0)
    node = row < count
    gain = jnp.where(node, jnp.exp2(jnp.log2(weight) * (-2.0 / 3.0)), 0.0)
    factor = jnp.where(row == 6, kernel_scale, -2.0 * gain)
    level = gain * (x * x + y * y + z * z + core_square)
    parts = []
    for value in (x * factor, y * factor, z * factor, gain):
        one, two, three = pieces(value)
        parts += [one, two, three, one, two, one]
    parts += list(pieces(level))
    parts += [jnp.zeros_like(x)] * (32 - len(parts))
    grid = jnp.concatenate(parts, 0).astype(jnp.bfloat16)
    offset = kernel_scale * (x[6:7, :] * x + y[6:7, :] * y + z[6:7, :] * z)
    return grid, offset


def work_body(
    count, begin, rows, tile, sub, info, near, rowgain, left, right, colgain, *refs
):
    keep, send, points, gain, grid_left, grid_right, off_left, off_right, dot_a, dot_b = refs[-10:]
    row_sign = info[1].astype(jnp.float32)
    col_sign = info[2].astype(jnp.float32)
    first_row = info[3]
    column = pl.program_id(0) * tile
    steps = rows // sub
    span = 2 * sub

    @pl.when(pl.program_id(0) == 0)
    def _():
        group = lax.broadcasted_iota(jnp.int32, (24, 256), 1) // 8
        source = lax.broadcasted_iota(jnp.int32, (24, 256), 0)
        spread = jnp.zeros((24, 256), jnp.float32)
        for slot, (piece, axis) in enumerate(SLOTS):
            spread = jnp.where((group == slot) & (source == 8 * piece + axis), 1.0, spread)
        pick = lax.broadcasted_iota(jnp.int32, (24, 128), 0)
        pick = jnp.where((pick == 5) | (pick == 13) | (pick == 21), 1.0, 0.0)
        lane = lax.broadcasted_iota(jnp.int32, (sub, 256), 1)
        place = lane - (lane // 8) * 8
        for half in range(2):
            x = near[half, 0:1, begin : begin + rows]
            y = near[half, 1:2, begin : begin + rows]
            z = near[half, 2:3, begin : begin + rows]
            own = rowgain[0, 0:1, begin : begin + rows] * 0.5
            zero = jnp.zeros_like(x)
            stack = [x, y, z, x * x + y * y + z * z, zero + 1.0, own, zero, zero]
            three = jnp.concatenate(pieces(jnp.concatenate(stack, 0)), 0)
            flat = jnp.transpose(three, (1, 0)).astype(jnp.bfloat16)
            wide = jnp.dot(
                flat, spread.astype(jnp.bfloat16), preferred_element_type=jnp.float32
            )
            if half == 0:
                gain[...] = jnp.dot(
                    flat, pick.astype(jnp.bfloat16), preferred_element_type=jnp.float32
                )
            for index in range(steps):
                block = wide[index * sub : (index + 1) * sub, :]
                for which in range(count + 1):
                    spot = which if which < count else 6
                    at = which * span + half * sub
                    points[index, at : at + sub, :] = jnp.where(
                        place == spot, block, 0.0
                    ).astype(jnp.bfloat16)

    grid, offset = panel_rows(count, left)
    grid_left[...] = grid
    off_left[...] = offset
    grid, offset = panel_rows(count, right)
    grid_right[...] = grid
    off_right[...] = offset

    def product(index, grid):
        return jnp.dot(points[index], grid[...], preferred_element_type=jnp.float32)

    def mix(dots, off):
        base = dots[count * span : (count + 1) * span, :]
        total = None
        for which in range(count):
            root = lax.rsqrt(dots[which * span : (which + 1) * span, :])
            term = (base - off[which : which + 1, :]) * (root * root * root)
            total = term if total is None else total + term
        return total[:sub] + row_sign * total[sub:]

    dot_a[...] = product(0, grid_left)

    def step(index, carry):
        at = pl.ds(pl.multiple_of(index * sub, sub), sub)
        dot_b[...] = product(index, grid_right)
        lift = gain[at, :]
        lift = jnp.concatenate([lift] * (tile // 128), 1)
        mixed_left = mix(dot_a, off_left) * lift
        dot_a[...] = product(jnp.minimum(index + 1, steps - 1), grid_left)
        mixed_right = mix(dot_b, off_right) * (lift * col_sign)
        keep[at, :] = (mixed_left + mixed_right) * colgain[...]
        send[at, :] = mixed_left - mixed_right
        return carry

    lax.fori_loop(0, steps, step, 0)

    @pl.when((column < first_row + rows) & (column + tile > first_row))
    def _():
        down = lax.broadcasted_iota(jnp.int32, (rows, tile), 0) + first_row
        over = lax.broadcasted_iota(jnp.int32, (rows, tile), 1) + column
        lift = jnp.concatenate([gain[...]] * (tile // 128), 1)
        spot = jnp.where(down == over, 0.5, 0.0) * lift
        turn = row_sign * col_sign
        keep[...] += spot * (1.0 + turn) * colgain[...]
        send[...] += spot * (1.0 - turn)


def work(count, info, near, rowgain, table, colgain, out, height, begin, end):
    rows = end - begin
    half = table.shape[1] // 2
    tile = math.gcd(half, 256)
    tiles = half // tile
    sub = math.gcd(rows, SUB)
    share = near.shape[2]
    lhs = (count + 1) * 2 * sub
    in_specs = [
        pl.BlockSpec((2, 3, share), lambda j, s: (0, 0, 0)),
        pl.BlockSpec((1, 1, share), lambda j, s: (s[4], 0, 0)),
        pl.BlockSpec((32, tile), lambda j, s: (0, j)),
        pl.BlockSpec((32, tile), lambda j, s: (0, j + tiles)),
        pl.BlockSpec((1, tile), lambda j, s: (0, j)),
    ]
    operands = [info, near, rowgain, table, table, colgain]
    alias = {}
    if out is not None:
        in_specs.append(pl.BlockSpec(memory_space=pl.ANY))
        alias = {len(operands): 0}
        operands.append(out)
    return pl.pallas_call(
        functools.partial(work_body, count, begin, rows, tile, sub),
        grid_spec=pltpu.PrefetchScalarGridSpec(
            num_scalar_prefetch=1,
            grid=(tiles,),
            in_specs=in_specs,
            out_specs=[
                pl.BlockSpec(
                    (pl.Element(rows), pl.Element(tile)),
                    lambda j, s: (pl.multiple_of(s[0] * 8, 8), j * tile),
                ),
                pl.BlockSpec((rows, tile), lambda j, s: (0, j)),
            ],
            scratch_shapes=[
                pltpu.VMEM((rows // sub, lhs, 256), jnp.bfloat16),
                pltpu.VMEM((rows, 128), jnp.float32),
                pltpu.VMEM((256, tile), jnp.bfloat16),
                pltpu.VMEM((256, tile), jnp.bfloat16),
                pltpu.VMEM((8, tile), jnp.float32),
                pltpu.VMEM((8, tile), jnp.float32),
                pltpu.VMEM((lhs, tile), jnp.float32),
                pltpu.VMEM((lhs, tile), jnp.float32),
            ],
        ),
        out_shape=[
            jax.ShapeDtypeStruct((height, half), jnp.float32),
            jax.ShapeDtypeStruct((rows, half), jnp.float32),
        ],
        input_output_aliases=alias,
        compiler_params=pltpu.CompilerParams(vmem_limit_bytes=LIMIT),
        cost_estimate=pl.CostEstimate(
            flops=rows * half * 4 * 7 * 512,
            bytes_accessed=rows * half * 8,
            transcendentals=rows * half * 4 * 6,
        ),
        name=f"work_{begin}",
    )(*operands)

def merge_body(info, got, colgain, _, out):
    out[...] = got[...] * colgain[...]


def merge(info, got, colgain, out):
    height, breadth = out.shape
    rows = got.shape[0]
    step = math.gcd(rows, 32)
    return pl.pallas_call(
        merge_body,
        grid_spec=pltpu.PrefetchScalarGridSpec(
            num_scalar_prefetch=1,
            grid=(rows // step,),
            in_specs=[
                pl.BlockSpec((step, breadth), lambda i, s: (i, 0)),
                pl.BlockSpec((1, breadth), lambda i, s: (0, 0)),
                pl.BlockSpec(memory_space=pl.ANY),
            ],
            out_specs=pl.BlockSpec(
                (pl.Element(step), pl.Element(breadth)),
                lambda i, s: (pl.multiple_of(s[0] * 8 + i * step, 8), 0),
            ),
        ),
        out_shape=jax.ShapeDtypeStruct(out.shape, jnp.float32),
        input_output_aliases={3: 0},
        compiler_params=pltpu.CompilerParams(vmem_limit_bytes=LIMIT),
        cost_estimate=pl.CostEstimate(
            flops=rows * breadth, bytes_accessed=rows * breadth * 8, transcendentals=0
        ),
        name="merge",
    )(info, got, colgain, out)


def per_device(centroids, normals, nodes, weights, row_scale, col_scale):
    rows = lax.axis_size("row")
    cores = lax.axis_size("col")
    row_pos = lax.axis_index("row")
    col_pos = lax.axis_index("col")
    half_row = rows // 2
    half_col = cores // 2
    height = row_scale.shape[0]
    breadth = col_scale.shape[0]
    count = weights.shape[0]
    share = height // 2
    table, near = gather(normals, nodes, weights, centroids)

    upper = row_pos < half_row
    low = lax.rem(row_pos, half_row)
    low_col = lax.rem(col_pos, half_col)
    core = col_pos // half_col
    if cores > 2:
        mine = lax.all_gather(centroids, "col", axis=1, tiled=True)
        hops = [(source, (source + half_row) % rows) for source in range(rows)]
        far = lax.ppermute(mine, "row", hops)
        near = jnp.stack([jnp.where(upper, mine, far), jnp.where(upper, far, mine)], 0)
        near = lax.dynamic_slice_in_dim(near, core * share, share, 2)
    rowgain = row_scale.reshape(2, 1, share)
    colgain = col_scale[None, :]

    unit = math.gcd(share, 64)
    blocks = share // unit
    front = (blocks * 4 + 6) // 7
    cuts = [(0, front * unit), (front * unit, share)]
    row_sign = jnp.where(upper, 1, -1)
    col_sign = jnp.where(core == 0, 1, -1)
    swap = [(source, (source + half_col) % cores) for source in range(cores)]
    out = None
    got = []
    for begin, end in cuts:
        where = core * share + begin
        first_row = low * height + where - low_col * breadth
        info = jnp.stack([where // 8, row_sign, col_sign, first_row, core]).astype(jnp.int32)
        out, send = work(
            count, info, near, rowgain, table, colgain, out, height, begin, end
        )
        got.append(lax.ppermute(send, "col", swap))
    for (begin, end), block in zip(cuts, got):
        where = (1 - core) * share + begin
        info = jnp.stack([where // 8]).astype(jnp.int32)
        out = merge(info, block, colgain, out)
    return out


def solution(mesh):
    placed = (
        P(None, ("row", "col")),
        P(None, ("col", "row")),
        P(None, ("col", "row")),
        P(None, ("col", "row")),
        P("row"),
        P("col"),
    )
    return jax.shard_map(
        per_device, mesh=mesh, in_specs=placed, out_specs=P("row", "col"), check_vma=False
    )
```

time: 413 us -> 205 us (0.50)
  the two profiles are of different devices: /device:TPU:0 before, /device:TPU:15 now
where the time goes in v1:
time: 205 us; the launch traced here: 204 us
  Pallas kernels  201 us (98%)
  local copies, waits for them, and re-layouts  2.6 us (1%)
    pallas_call x2, Pallas kernels, work(): pl.pallas_call(functools.partial(work_body, count, begin, rows, tile, sub...  153 us
    pallas_call x1, Pallas kernels, gather(): pl.pallas_call(functools.partial(gather_body, rows, cores), out_shape=[ja...  32.9 us
    pallas_call x2, Pallas kernels, merge(): pl.pallas_call(merge_body, grid_spec=pltpu.PrefetchScalarGridSpec(num_sca...  14.9 us
  transfers between devices with their start and end apart: 2, of which 1 were waited for; matrix products, arithmetic and copies ran while one was open for 0% of the time, Pallas kernels for 37%

profile of v1, /device:TPU:15, one launch (start us, length us, event | category | flops | bytes accessed | tf_op | source)
XLA Modules:
  0.0 204.4 jit_solution(4050019814431064576)
XLA Ops:
  0.0 1.3 reshape.3.rowgain
  1.3 32.9 %gather.1 = (f32[32,14336]{1,0:T(8,128)}, f32[2,3,448]{2,1,0:T(4,128)}) custom-call(f32[3,448]{1,0:T(4,128)} %normals.1, f32[18,448]{1,0:T(8,128)} %nodes.1, f32[6,448]{1,0:T(8,128)} %weights.1, f32[3,448]{1,0:T(4,128)} %centroids.1), custom_call_target="tpu_custom_call" | custom-call | tf_op jit(solution)/shard_map/gather/pallas_call | solution.py:104
  34.2 0.7 stack.45.info
  34.9 85.8 %work_0.1 = (f32[896,7168]{1,0:T(8,128)}, f32[256,7168]{1,0:T(8,128)}) custom-call(s32[5]{0:T(128)} %stack.45.info, f32[2,3,448]{2,1,0:T(4,128)} %get-tuple-element.11.near, f32[2,1,448]{2,1,0:T(1,128)} %reshape.3.rowgain, f32[32,14336]{1,0:T(8,128)} %get-tuple-element.12.left.right, f32[32,14336]{1,0:T(8,128)} %get-tuple-element.12.left.right, ...), custom_call_target="tpu_custom_call" | custom-call | flops 26306674688 | bytes 14680064 | tf_op jit(solution)/shard_map/work_0/pallas_call | solution.py:266
  120.7 0.1 collective-permute-start.1
  120.8 0.6 stack.42.info
  121.4 67.2 %work_256.1 = (f32[896,7168]{1,0:T(8,128)}, f32[192,7168]{1,0:T(8,128)}) custom-call(s32[5]{0:T(128)} %stack.42.info, f32[2,3,448]{2,1,0:T(4,128)} %get-tuple-element.11.near, f32[2,1,448]{2,1,0:T(1,128)} %reshape.3.rowgain, f32[32,14336]{1,0:T(8,128)} %get-tuple-element.12.left.right, ...), custom_call_target="tpu_custom_call", output_to_operand_aliasing={{0}: (6, {})} | custom-call | flops 19730006016 | bytes 11010048 | tf_op jit(solution)/shard_map/work_256/pallas_call | solution.py:266
  188.6 0.4 collective-permute-start
  189.0 0.0 collective-permute-done.1.got
  189.0 8.4 %merge.2._ = f32[896,7168]{1,0:T(8,128)} custom-call(s32[1]{0:T(128)} %bitcast.9.info, f32[256,7168]{1,0:T(8,128)} %collective-permute-done.1.got, f32[1,7168]{1,0:T(1,128)} %bitcast.12, f32[896,7168]{1,0:T(8,128)} %get-tuple-element.16._), custom_call_target="tpu_custom_call", output_to_operand_aliasing={{}: (3, {})} | custom-call | flops 1835008 | bytes 14680064 | tf_op jit(solution)/shard_map/merge/pallas_call | solution.py:312
  197.4 0.6 collective-permute-done.got
  198.0 6.5 %merge.3 = f32[896,7168]{1,0:T(8,128)} custom-call(s32[1]{0:T(128)} %bitcast.info, f32[192,7168]{1,0:T(8,128)} %collective-permute-done.got, f32[1,7168]{1,0:T(1,128)} %bitcast.13, f32[896,7168]{1,0:T(8,128)} %merge.2._), custom_call_target="tpu_custom_call", output_to_operand_aliasing={{}: (3, {})} | custom-call | flops 1376256 | bytes 11010048 | tf_op jit(solution)/shard_map/merge/pallas_call | solution.py:312
Async XLA Ops:
  120.7 68.3 %collective-permute-start.1 = (f32[256,7168]{1,0:T(8,128)}, f32[256,7168]{1,0:T(8,128)}, u32[]{:S(2)}, u32[]{:S(2)}) collective-permute-start(f32[256,7168]{1,0:T(8,128)} %get-tuple-element.15), channel_id=1, source_target_pairs={{0,1},{1,0},{2,3},{3,2},{4,5},{5,4},{6,7},{7,6},{8,9},{9,8},{10,11... | collective-permute-start | bytes 22020104 | tf_op jit(solution)/shard_map/ppermute | solution.py:379
  188.6 9.4 %collective-permute-start = (f32[192,7168]{1,0:T(8,128)}, f32[192,7168]{1,0:T(8,128)}, u32[]{:S(2)}, u32[]{:S(2)}) collective-permute-start(f32[192,7168]{1,0:T(8,128)} %get-tuple-element.14), channel_id=1, source_target_pairs={{0,1},{1,0},{2,3},{3,2},{4,5},{5,4},{6,7},{7,6},{8,9},{9,8},{10,11... | collective-permute-start | bytes 16515080 | tf_op jit(solution)/shard_map/ppermute | solution.py:379
